TPU v7x, 256 devices: a 8x8x2 block of a 8x8x16 slice. The times are simulated.
256 devices in a mesh: rep: 2 (over z), exp: 8 (over x), ten: 16 (over y, core).
Axes of the slice: x: 8, y: 8, z: 2, core: 2. Of those that a mesh axis runs over, the one named last changes fastest.
The devices are a block of a 8x8x16 slice.
Arguments:
- hidden_in: bfloat16 [6144, 3072], P(('rep', 'exp', 'ten')), parts along dimension 0, may hold values from -6 to 6
- queries: bfloat16 [6144, 6144], P(('rep', 'exp', 'ten')), parts along dimension 0, may hold values from -100 to 100
- new_kv: bfloat16 [2, 6144, 1024], P(None, ('rep', 'exp', 'ten')), parts along dimension 1, may hold values from -5 to 5
- prefix_kv: bfloat16 [2, 16, 512, 1024], P(None, ('rep', 'exp'), 'ten'), parts along dimension 1, may hold values from -5 to 5
- decode_kv: bfloat16 [2, 1024, 48, 1024], P(None, ('rep', 'exp', 'ten')), parts along dimension 1, may hold values from -5 to 5
- prefix_len: int32 [16], P(('rep', 'exp')), parts along dimension 0, may hold values from 2 to 512
- decode_len: int32 [1024], P(('rep', 'exp', 'ten')), parts along dimension 0, may hold values from 2 to 48
- out_proj: bfloat16 [6144, 3072], P('ten'), may hold values from -0.078125 to 0.078125
- norm_gain: float32 [3072], replicated, may hold values from 0.5 to 1.5
- router_w: bfloat16 [3072, 8], replicated, may hold values from -0.109375 to 0.109375
- expert_ids: int32 [6144, 2], P(('rep', 'exp', 'ten')), parts along dimension 0, may hold values from 0 to 7, all different within a row; in each aligned block of 24 rows (0 to 23, 24 to 47, ...) at most 7 rows name the same one
- w_gate: bfloat16 [8, 3072, 8192], P('exp', None, 'ten'), may hold values from -0.109375 to 0.109375
- w_up: bfloat16 [8, 3072, 8192], P('exp', None, 'ten'), may hold values from -0.109375 to 0.109375
- w_down: bfloat16 [8, 8192, 3072], P('exp', 'ten'), may hold values from -0.0625 to 0.0625
Outputs:
- layer_out: bfloat16 [6144, 3072], P(('rep', 'exp', 'ten')), parts along dimension 0
There are 2 independent parts, one for each index of `rep`. A program takes and returns all parts, laid end to end along the dimension named above; an argument that names none is the same for every part. Nothing has to cross between parts.
Inputs may be any that keep to these rules, and one draw needn't show every extreme that they name: `expert_ids`: each row names two different experts. Within each aligned block of 24 rows (the rows of one device) no expert is named by more than 7 rows, and in some block one expert is named by exactly 7 rows.
All inputs are finite; a program needn't handle non-finite values.
Results may differ from a plain program's by a relative error of at most 0.013.
Values may be sent and summed in bfloat16 or wider, within the bound.
A program may use at most 128 MiB of HBM per device.

v0:
```python
import jax
import jax.numpy as jnp
from jax import lax
from jax.sharding import Mesh
from jax.sharding import PartitionSpec as P

HD = 128
CAP = 7
TEN = ("ten_0", "ten_1")
REP_EXP_TEN = ("rep", "exp", "ten_0", "ten_1")


lowest_score = -1e30


def in_order(parts, dim):
    parts = jnp.moveaxis(parts, 0, dim)
    lengths = parts.shape
    return parts.reshape(*lengths[:dim], lengths[dim] * lengths[dim + 1], *lengths[dim + 2 :])


def one_gather(arrays, axis, dims):
    line = jnp.concatenate([a.reshape(-1) for a in arrays])
    lines, at, done = (lax.all_gather(line, axis), 0, [])
    for a, dim in zip(arrays, dims):
        parts = lines[:, at : at + a.size].reshape(-1, *a.shape)
        done.append(in_order(parts, dim))
        at += a.size
    return tuple(done)


def split_up(shard, dim, length):
    lengths = shard.shape
    parts = shard.reshape(*lengths[:dim], length, lengths[dim] // length, *lengths[dim + 1 :])
    return jnp.moveaxis(parts, dim, 0)


def sum_by_chip(shard, chips, core, dim):
    sizes = (lax.axis_size(chips), lax.axis_size(core))
    parts = split_up(shard, dim, sizes[0] * sizes[1])
    inside = parts.shape[1:]
    parts = parts.reshape(*sizes, *inside).swapaxes(0, 1).reshape(-1, *inside)
    parts = lax.psum_scatter(parts, core, scatter_dimension=0, tiled=True)
    return lax.psum_scatter(parts, chips, scatter_dimension=0, tiled=True)[0]


def local_softmax(scores, visible):
    masked = jnp.where(visible, scores, lowest_score)
    row_max = jnp.max(masked, axis=-1)
    exponent = jnp.where(visible, jnp.exp(masked - row_max[..., None]), 0.0)
    return (row_max, exponent, jnp.sum(exponent, axis=-1))


def on_device(
    hidden_in,
    queries,
    new_kv,
    prefix_kv,
    decode_kv,
    prefix_len,
    decode_len,
    out_proj,
    norm_gain,
    router_w,
    expert_ids,
    w_gate,
    w_up,
    w_down,
):
    ten_size = lax.axis_size(TEN)
    groups = lax.axis_size("exp")
    my_ten = lax.axis_index(TEN)
    rows_dev, model_width = hidden_in.shape
    dec_dev = decode_len.shape[0]
    span_dev = rows_dev - dec_dev
    span_rows = span_dev * ten_size
    kv_width = new_kv.shape[2]
    heads_kv = kv_width // HD
    heads_q = queries.shape[1] // HD
    per_kv = heads_q // heads_kv
    score_scale = HD ** (-0.5)
    ctx_len = decode_kv.shape[2]
    own_heads = queries.reshape(rows_dev, heads_kv, per_kv, HD)
    dec_keys = jnp.concatenate([decode_kv[0], new_kv[0, span_dev:, None]], axis=1).reshape(
        dec_dev, ctx_len + 1, heads_kv, HD
    )
    dec_values = jnp.concatenate([decode_kv[1], new_kv[1, span_dev:, None]], axis=1).reshape(
        dec_dev, ctx_len + 1, heads_kv, HD
    )
    dec_scores = (
        jnp.einsum(
            "dcgh,dpch->dcgp", own_heads[span_dev:], dec_keys, preferred_element_type=jnp.float32
        )
        * score_scale
    )
    dec_pos = jnp.arange(ctx_len + 1, dtype=jnp.int32)[None, :]
    dec_visible = ((dec_pos < decode_len[:, None]) | (dec_pos == ctx_len))[:, None, None, :]
    dec_max, dec_exponent, dec_totals = local_softmax(dec_scores, dec_visible)
    dec_partial = jnp.einsum(
        "dcgp,dpch->dcgh",
        dec_exponent.astype(jnp.bfloat16),
        dec_values,
        preferred_element_type=jnp.float32,
    )
    full_prefix, full_fresh = one_gather((prefix_kv[:, 0], new_kv[:, :span_dev]), TEN, (1, 1))
    prefix_total = full_prefix.shape[1]
    key_rows = jnp.concatenate([full_prefix[0], full_fresh[0]], axis=0).reshape(
        prefix_total + span_rows, heads_kv, HD
    )
    value_rows = jnp.concatenate([full_prefix[1], full_fresh[1]], axis=0).reshape(
        prefix_total + span_rows, heads_kv, HD
    )
    scores = (
        jnp.einsum(
            "rcgh,pch->rcgp", own_heads[:span_dev], key_rows, preferred_element_type=jnp.float32
        )
        * score_scale
    )
    query_row = my_ten * span_dev + jnp.arange(span_dev, dtype=jnp.int32)[:, None]
    positions = jnp.arange(prefix_total + span_rows, dtype=jnp.int32)[None, :]
    visible = jnp.where(
        positions < prefix_total, positions < prefix_len[0], positions - prefix_total <= query_row
    )[:, None, None, :]
    row_max, exponent, totals = local_softmax(scores, visible)
    span_out = (
        jnp.einsum(
            "rcgp,pch->rcgh",
            exponent.astype(jnp.bfloat16),
            value_rows,
            preferred_element_type=jnp.float32,
        )
        / totals[..., None]
    )
    dec_out = dec_partial / dec_totals[..., None]
    attended_rows = (
        jnp.concatenate([span_out, dec_out], axis=0)
        .reshape(rows_dev, heads_q * HD)
        .astype(jnp.bfloat16)
    )
    attended = lax.all_to_all(attended_rows, TEN, split_axis=1, concat_axis=0, tiled=True)
    row_block = attended
    projected = sum_by_chip(
        jnp.dot(row_block, out_proj, preferred_element_type=jnp.float32).astype(jnp.bfloat16),
        "ten_0",
        "ten_1",
        0,
    ).astype(jnp.float32)
    residual = hidden_in.astype(jnp.float32) + projected
    mean_square = jnp.mean(residual * residual, axis=1, keepdims=True)
    normed = (residual * lax.rsqrt(mean_square + 1e-05) * norm_gain).astype(jnp.bfloat16)
    logits = jnp.dot(normed, router_w, preferred_element_type=jnp.float32)
    experts = router_w.shape[1]
    chosen_hot = (expert_ids[:, :, None] == jnp.arange(experts, dtype=jnp.int32)).astype(jnp.int32)
    chosen_logits = jnp.sum(jnp.where(chosen_hot == 1, logits[:, None, :], 0.0), axis=2)
    route_weights = jax.nn.softmax(chosen_logits, axis=1)
    flat_hot = chosen_hot.reshape(rows_dev * 2, experts)
    slot_rank = jnp.sum((jnp.cumsum(flat_hot, axis=0) - flat_hot) * flat_hot, axis=1).reshape(
        rows_dev, 2
    )
    capacity = CAP
    slot_index = jnp.arange(capacity, dtype=jnp.int32)
    assignment = chosen_hot[:, :, :, None] * (slot_rank[:, :, None, None] == slot_index).astype(
        jnp.int32
    )
    placement = jnp.sum(assignment, axis=1)
    local_experts = experts // groups
    placement_split = placement.reshape(rows_dev, groups, local_experts, capacity).astype(
        jnp.bfloat16
    )
    outgoing = jnp.einsum(
        "rnlc,rd->lncd", placement_split, normed, preferred_element_type=jnp.float32
    ).astype(jnp.bfloat16)
    arrived = lax.all_to_all(outgoing, "exp", split_axis=1, concat_axis=1, tiled=True)
    shard_rows = lax.all_gather(arrived, TEN, axis=1, tiled=True)
    gate_act = jnp.einsum("lscd,ldf->lscf", shard_rows, w_gate, preferred_element_type=jnp.float32)
    up_act = jnp.einsum("lscd,ldf->lscf", shard_rows, w_up, preferred_element_type=jnp.float32)
    hidden = (jax.nn.silu(gate_act) * up_act).astype(jnp.bfloat16)
    row_block = hidden
    summed = lax.psum_scatter(
        jnp.einsum("lscf,lfd->slcd", row_block, w_down, preferred_element_type=jnp.float32).astype(
            jnp.bfloat16
        ),
        TEN,
        scatter_dimension=0,
        tiled=True,
    )
    returned = lax.all_to_all(summed, "exp", split_axis=0, concat_axis=0, tiled=True)
    outputs = returned.reshape(experts * capacity, model_width).astype(jnp.float32)
    weight_map = jnp.sum(
        assignment.astype(jnp.float32) * route_weights[:, :, None, None], axis=1
    ).reshape(rows_dev, experts * capacity)
    expert_mix = jnp.dot(weight_map, outputs, preferred_element_type=jnp.float32)
    return (residual + expert_mix).astype(jnp.bfloat16)


def solution(mesh):
    split = Mesh(
        mesh.devices.reshape(mesh.shape["rep"], mesh.shape["exp"], 8, 2),
        ("rep", "exp", "ten_0", "ten_1"),
    )
    return jax.shard_map(
        on_device,
        mesh=split,
        in_specs=(
            P(REP_EXP_TEN, None),
            P(REP_EXP_TEN, None),
            P(None, REP_EXP_TEN, None),
            P(None, ("rep", "exp"), TEN, None),
            P(None, REP_EXP_TEN, None, None),
            P(("rep", "exp")),
            P(REP_EXP_TEN),
            P(TEN, None),
            P(),
            P(),
            P(REP_EXP_TEN, None),
            P("exp", None, TEN),
            P("exp", None, TEN),
            P("exp", TEN, None),
        ),
        out_specs=P(REP_EXP_TEN, None),
        check_vma=False,
    )
```

profile of v0, /device:TPU:513, one launch (start us, length us, event | category | flops | bytes accessed | tf_op | source)
XLA Modules:
  0.0 359.8 jit_solution(4023740296846437345)
XLA Ops:
  6.6 1.1 reshape.257
  7.7 0.9 copy.98
  11.5 0.9 slice.60
  12.5 1.3 slice.57
  13.8 1.2 fusion.94
  15.0 0.8 copy.79
  17.3 2.1 fusion.96
  19.5 0.8 copy.83
  21.0 2.4 fusion.47
  23.4 1.0 fusion.53
  24.4 46.6 %all-gather.6.cloned.1.call-done = bf16[1703936]{0:T(1024)(128)(2,1)} async-done(((bf16[106496]{0:T(1024)(128)(2,1)}), bf16[1703936]{0:T(1024)(128)(2,1)}) %all-gather.6.cloned.1.call-update) | async-done | bytes 3407888 | tf_op jit(solution)/shard_map/all_gather | solution.py:24
  71.1 4.2 %reshape.268 = bf16[16,106496]{1,0:T(8,128)(2,1)} reshape(bf16[1703936]{0:T(1024)(128)(2,1)} %all-gather.6.cloned.1.call-done) | data formatting | bytes 6815744 | tf_op jit(solution)/shard_map/all_gather | solution.py:24
  75.2 2.6 slice.66
  77.8 1.2 copy.99
  79.5 1.1 copy.74
  80.9 1.2 copy.76
  82.1 2.9 reshape.259
  84.9 2.6 fusion.93
  87.6 2.2 concatenate.41
  89.8 2.0 copy.75
  91.8 2.2 concatenate.44
  94.0 1.2 copy.77
  95.2 2.4 fusion.19
  97.7 1.9 fusion.99
  100.6 0.9 convert_element_type.85
  101.5 1.0 copy.86
  102.5 16.7 %all_to_all.26 = bf16[24,16,384]{2,0,1:T(8,128)(2,1)S(1)} all-to-all(bf16[24,16,384]{2,0,1:T(8,128)(2,1)S(1)} %copy.86), channel_id=1, replica_groups=mesh['rep'=2,'exp'=8,'ten_0'=8,'ten_1'=2] {'ten_0','ten_1'}, dimensions={1} | all-to-all | bytes 589824 | tf_op jit(solution)/shard_map/all_to_all | solution.py:140
  119.2 3.1 convolution_convert_fusion
  122.3 1.6 copy.87
  124.1 14.4 %reduce-scatter.6.cloned.1.call-done = bf16[8,24,3072]{2,1,0:T(8,128)(2,1)} async-done(((bf16[16,24,3072]{2,1,0:T(8,128)(2,1)}), bf16[8,24,3072]{2,1,0:T(8,128)(2,1)}) %reduce-scatter.6.cloned.1.call-update) | async-done | bytes 1179664 | tf_op jit(solution)/shard_map/reduce_scatter | solution.py:43
  139.3 38.8 %reduce-scatter.8.cloned.1.call-done = bf16[1,24,3072]{2,1,0:T(8,128)(2,1)} async-done(((bf16[8,24,3072]{2,1,0:T(8,128)(2,1)}), bf16[1,24,3072]{2,1,0:T(8,128)(2,1)}) %reduce-scatter.8.cloned.1.call-update) | async-done | bytes 147472 | tf_op jit(solution)/shard_map/reduce_scatter | solution.py:44
  178.1 1.1 multiply_reduce_fusion
  179.2 1.0 multiply_convert_fusion.1
  181.3 17.1 %all_to_all.27 = bf16[1,8,7,3072]{3,2,0,1:T(8,128)(2,1)S(1)} all-to-all(bf16[1,8,7,3072]{3,2,0,1:T(8,128)(2,1)S(1)} %copy.91), channel_id=1, replica_groups=mesh['rep'=2,'exp'=8,'ten_0'=8,'ten_1'=2] {'exp'}, dimensions={1} | all-to-all | bytes 688128 | tf_op jit(solution)/shard_map/all_to_all | solution.py:173
  198.4 1.0 copy.92
  199.5 45.3 %all-gather.4.cloned.1.call-done = bf16[1,128,7,3072]{3,1,2,0:T(8,128)(2,1)} async-done(((bf16[1,8,7,3072]{3,1,2,0:T(8,128)(2,1)}), bf16[1,128,7,3072]{3,1,2,0:T(8,128)(2,1)}) %all-gather.4.cloned.1.call-update) | async-done | bytes 5505040 | tf_op jit(solution)/shard_map/all_gather | solution.py:174
  244.8 7.8 %fusion.4 = f32[128,7,512]{2,0,1:T(8,128)} fusion(bf16[1,128,7,3072]{3,1,2,0:T(8,128)(2,1)} %all-gather.4.cloned.1.call-done, bf16[1,3072,512]{2,1,0:T(8,128)(2,1)} %param.25), kind=kOutput, calls=%fused_computation.4 | convolution fusion | flops 2818572288 | bytes 10485760 | tf_op jit(solution)/shard_map/lscd,ldf->lscf/dot_general | solution.py:175
  252.6 10.9 %fusion.100 = bf16[16,8,7,3072]{3,1,0,2:T(8,128)(2,1)} fusion(bf16[1,512,3072]{2,1,0:T(8,128)(2,1)S(1)} %copy-done, f32[128,7,512]{2,0,1:T(8,128)} %fusion.4, bf16[1,3072,512]{2,1,0:T(8,128)(2,1)} %param.26, bf16[1,128,7,3072]{3,1,2,0:T(8,128)(2,1)} %all-gather.4.cloned.1.call-done), kind=kOutput, calls=%fused_computation.103 | convolution fusion | flops 5642649600 | bytes 19136512 | tf_op jit(solution)/shard_map/lscf,lfd->slcd/dot_general | solution.py:180
  263.4 5.3 %copy.104 = bf16[16,8,7,3072]{3,1,2,0:T(8,128)(2,1)} copy(bf16[16,8,7,3072]{3,1,0,2:T(8,128)(2,1)} %fusion.100) | data formatting | bytes 11010048
  268.8 63.1 %reduce-scatter.10.cloned.1.call-done = bf16[8,21504]{1,0:T(8,128)(2,1)} async-done(((bf16[128,21504]{1,0:T(8,128)(2,1)}), bf16[8,21504]{1,0:T(8,128)(2,1)}) %reduce-scatter.10.cloned.1.call-update) | async-done | bytes 344080
  331.9 1.9 copy.93
  333.9 5.8 %all-to-all-start.2 = ((bf16[8,1,7,3072]{3,2,1,0:T(8,128)(2,1)}), bf16[8,1,7,3072]{3,2,1,0:T(8,128)(2,1)S(1)}, u32[]{:S(2)}, u32[]{:S(2)}) async-start(bf16[8,1,7,3072]{3,2,1,0:T(8,128)(2,1)} %copy.93), calls=%async_computation.4 | async-start | bytes 786432 | tf_op jit(solution)/shard_map/all_to_all | solution.py:187
  339.6 1.1 fusion.107
  340.7 1.3 select_reduce_fusion.1
  342.0 1.3 reduce_max.29
  345.3 5.1 %all-to-all-done.2 = bf16[8,1,7,3072]{3,2,1,0:T(8,128)(2,1)S(1)} async-done(((bf16[8,1,7,3072]{3,2,1,0:T(8,128)(2,1)}), bf16[8,1,7,3072]{3,2,1,0:T(8,128)(2,1)S(1)}, u32[]{:S(2)}, u32[]{:S(2)}) %all-to-all-start.2) | async-done | bytes 344096 | tf_op jit(solution)/shard_map/all_to_all | solution.py:187
  350.4 0.8 reshape.266
  351.3 2.0 fusion.7
  (72 shorter events, 10.4 us)
Async XLA Ops:
  6.5 246.0 %copy-start = (bf16[1,512,3072]{2,1,0:T(8,128)(2,1)S(1)}, bf16[1,512,3072]{2,1,0:T(8,128)(2,1)}, u32[]{:S(2)}) copy-start(bf16[1,512,3072]{2,1,0:T(8,128)(2,1)} %param.27) | copy-start | bytes 9437188
  6.6 64.5 %all-gather.6.cloned.1.call-start = ((), (), s32[]{:S(2)}) async-start(), calls=%async_computation.9 | async-start | bytes 3620864 | tf_op jit(solution)/shard_map/all_gather | solution.py:24
  9.3 129.1 %reduce-scatter.6.cloned.1.call-start = ((), (), s32[]{:S(2)}) async-start(), calls=%async_computation.6 | async-start | bytes 3538944 | tf_op jit(solution)/shard_map/reduce_scatter | solution.py:43
  10.8 6.5 %copy-start.7 = (bf16[4,1,8,128]{3,1,2,0:T(2,128)(2,1)}, bf16[4,1,8,128]{3,1,2,0:T(2,128)(2,1)S(1)}, u32[]{:S(2)}) copy-start(bf16[4,1,8,128]{3,1,2,0:T(2,128)(2,1)S(1)} %concatenate.53) | copy-start | bytes 24580
  12.4 4.9 %copy-start.5 = (bf16[4,8,6,128]{3,2,1,0:T(8,128)(2,1)}, bf16[4,8,6,128]{3,2,1,0:T(8,128)(2,1)S(1)}, u32[]{:S(2)}) copy-start(bf16[4,8,6,128]{3,2,1,0:T(8,128)(2,1)S(1)} %slice.61) | copy-start | bytes 147460
  13.8 3.0 copy-start.10
  75.2 2.6 slice-start
  95.2 2.5 copy-start.6
  97.7 1.9 copy-start.3
  97.7 1.9 copy-start.4
  122.3 16.3 %copy-start.9 = (s32[24,2]{0,1:T(2,128)S(1)}, s32[24,2]{0,1:T(2,128)}, u32[]{:S(2)}) copy-start(s32[24,2]{0,1:T(2,128)} %param.24) | copy-start | bytes 580
  122.3 55.8 %copy-start.1 = (bf16[24,3072]{1,0:T(8,128)(2,1)S(1)}, bf16[24,3072]{1,0:T(8,128)(2,1)}, u32[]{:S(2)}) copy-start(bf16[24,3072]{1,0:T(8,128)(2,1)} %param.14) | copy-start | bytes 442372
  123.9 55.2 %copy-start.8 = (f32[3072]{0:T(1024)S(1)}, f32[3072]{0:T(1024)}, u32[]{:S(2)}) copy-start(f32[3072]{0:T(1024)} %param.22) | copy-start | bytes 36868
  124.0 54.1 %reduce-scatter.8.cloned.1.call-start = ((), (), s32[]{:S(2)}) async-start(), calls=%async_computation.7 | async-start | bytes 1327104 | tf_op jit(solution)/shard_map/reduce_scatter | solution.py:44
  138.5 106.3 %all-gather.4.cloned.1.call-start = ((), (), s32[]{:S(2)}) async-start(), calls=%async_computation.8 | async-start | bytes 5849088 | tf_op jit(solution)/shard_map/all_gather | solution.py:174
  180.2 0.7 copy-start.2
  199.5 132.5 %reduce-scatter.10.cloned.1.call-start = ((), (), s32[]{:S(2)}) async-start(), calls=%async_computation.10 | async-start | bytes 5849088
  333.9 16.6 %all-to-all-start.2 = ((bf16[8,1,7,3072]{3,2,1,0:T(8,128)(2,1)}), bf16[8,1,7,3072]{3,2,1,0:T(8,128)(2,1)S(1)}, u32[]{:S(2)}, u32[]{:S(2)}) async-start(bf16[8,1,7,3072]{3,2,1,0:T(8,128)(2,1)} %copy.93), calls=%async_computation.4 | async-start | bytes 786432 | tf_op jit(solution)/shard_map/all_to_all | solution.py:187
Sparse Core Ops, SparseCore 0:
  9.5 61.5 all-gather.5
  124.1 14.2 reduce-scatter.5
  141.0 37.0 reduce-scatter.7
  199.6 45.1 all-gather.3
  268.9 62.9 reduce-scatter.9
where the time goes:
time: 363 us; the launch traced here: 360 us
  waiting for transfers between devices  214 us (59%)
  local copies, waits for them, and re-layouts  48.2 us (13%)
  blocking collectives  33.9 us (9%)
  matrix products  32.7 us (9%)
  between operations  14.1 us (4%)
  other arithmetic  11.4 us (3%)
  starting transfers between devices  6.03 us (2%)
    unnamed x6, waiting for transfers between devices  63.4 us
    all_gather x1, waiting for transfers between devices, one_gather(): lines, at, done = (lax.all_gather(line, axis), 0, [])  46.6 us
    all_gather x1, waiting for transfers between devices, on_device(): shard_rows = lax.all_gather(arrived, TEN, axis=1, tiled=True)  45.3 us
    reduce_scatter x1, waiting for transfers between devices, sum_by_chip(): return lax.psum_scatter(parts, chips, scatter_dimension=0, tiled=True)[0]  38.8 us
    all_to_all x1, blocking collectives, on_device(): lax.all_to_all(outgoing, 'exp', split_axis=1, concat_axis=1, tiled=True)  17.1 us
    all_to_all x1, blocking collectives, on_device(): lax.all_to_all(attended_rows, TEN, split_axis=1, concat_axis=0, tiled=True)  16.7 us
    reduce_scatter x1, waiting for transfers between devices, sum_by_chip(): parts = lax.psum_scatter(parts, core, scatter_dimension=0, tiled=True)  14.4 us
    dot_general x1, matrix products, on_device(): jnp.einsum('lscf,lfd->slcd', row_block, w_down, preferred_element_type=jn...  10.9 us
  transfers between devices with their start and end apart: 6, of which 6 were waited for; matrix products, arithmetic and copies ran while one was open for 6% of the time, Pallas kernels for 0%

commit v1 on v0

v1 whole, which is shorter than its diff:
```python
import jax
import jax.numpy as jnp
from jax import lax
from jax.experimental import pallas as pl
from jax.experimental.pallas import tpu as pltpu
from jax.sharding import Mesh
from jax.sharding import PartitionSpec as P

MESH = pl.DeviceIdType.MESH
HD = 128
CAP = 7
F32 = jnp.float32
BF16 = jnp.bfloat16
NEG = -1e30
EXP, CHIP, CORE = "exp", "ten_0", "ten_1"
TEN = (CHIP, CORE)
REP_EXP_TEN = ("rep", EXP, CHIP, CORE)


def iota(shape, dim):
    return lax.broadcasted_iota(jnp.int32, shape, dim)


def cols(start, size):
    return pl.ds(pl.multiple_of(start, 128), size)


def rows(start, size, align):
    return pl.ds(pl.multiple_of(start, align), size)


def dot(a, b):
    return jnp.dot(a, b, preferred_element_type=F32)


def dot_t(a, b):
    return lax.dot_general(a, b, (((1,), (1,)), ((), ())), preferred_element_type=F32)


def ring_order(chips):
    far = chips // 2
    order = []
    for hop in range(far - 1, 0, -1):
        order += [(False, hop), (True, hop + 1)]
    return order + [(True, 1)]


class Copies:
    def __init__(self):
        self.sent = []

    def start(self, copy):
        copy.start()
        self.sent.append(copy)
        return copy

    def drain(self):
        for copy in self.sent:
            copy.wait_send()
        self.sent = []


def remote(src, dst, send_sem, recv_sem, **device):
    return pltpu.make_async_remote_copy(
        src_ref=src, dst_ref=dst, send_sem=send_sem, recv_sem=recv_sem,
        device_id=device, device_id_type=MESH,
    )


def ring_reduce(y, chips, copies, part, rs_out, rs_in, s_sem, r_sem, subs):
    order = ring_order(chips)
    place = {m: i for i, m in enumerate(order)}

    def copy(way, index, sub):
        to = lax.rem(y + (1 if way == 0 else chips - 1), chips)
        return remote(
            rs_out.at[way, index, sub], rs_in.at[way, index, sub],
            s_sem.at[way, index, sub], r_sem.at[way, index, sub], **{CHIP: to},
        )

    for index, (is_long, hop) in enumerate(order):
        for sub in range(subs):
            for way in range(2):
                half = (0 if is_long else 1) ^ way
                dest = lax.rem(y + (hop if way == 0 else chips - hop), chips)
                value = part(dest, half, sub)
                if (is_long, hop + 1) in place:
                    before = place[is_long, hop + 1]
                    copy(way, before, sub).wait_recv()
                    value = value + rs_in[way, before, sub].astype(F32)
                rs_out[way, index, sub] = value.astype(BF16)
                copies.start(copy(way, index, sub))

    def total(half, sub):
        value = part(y, half, sub)
        for way in range(2):
            last = place[(half ^ way) == 0, 1]
            copy(way, last, sub).wait_recv()
            value = value + rs_in[way, last, sub].astype(F32)
        return value

    return total


def k1_scratch(d):
    r, c, n = d["rows"], d["chips"], 2 * d["chips"]
    jw = d["heads_dev"] * HD
    half = d["model"] // 2
    msgs = len(ring_order(c))
    v, dma = pltpu.VMEM, pltpu.SemaphoreType.DMA
    return dict(
        q_v=v((r, d["heads_q"] * HD), BF16),
        nkv_v=v((2, r, d["kvw"]), BF16),
        pre_v=v((2, d["pre_dev"], d["kvw"]), BF16),
        dec_v=v((2, d["dec"], d["ctx"], d["kvw"]), BF16),
        qb=v((n, r, jw), BF16),
        kvn=v((2, c, 2, r, HD), BF16),
        kvp=v((2, c, 2, d["pre_dev"], HD), BF16),
        dec_o=v((d["heads_q"] * 8, HD), BF16),
        decs=v((n, 16, HD), BF16),
        decr=v((n, 16, HD), BF16),
        qh=v((d["heads_dev"] * n * r, HD), BF16),
        kall=v((n * (d["pre_dev"] + r), HD), BF16),
        vall=v((n * (d["pre_dev"] + r), HD), BF16),
        att=v((2, n * r, jw), BF16),
        wo=v((2, jw, half), BF16),
        part=v((n * r, half), F32),
        rs_out=v((2, msgs, 1, 2 * r, half // 2), BF16),
        rs_in=v((2, msgs, 1, 2 * r, half // 2), BF16),
        l_sem=dma((9,)),
        qs_sem=dma((n,)),
        qr_sem=dma((n,)),
        kns_sem=dma((c,)),
        knr_sem=dma((c,)),
        kps_sem=dma((c,)),
        kpr_sem=dma((c,)),
        x_s=dma((8,)),
        x_r=dma((8,)),
        ds_sem=dma((n,)),
        dr_sem=dma((n,)),
        rs_s=dma((2, msgs, 1)),
        rs_r=dma((2, msgs, 1)),
    )


def attend_and_project(d, S, y, k, copies, q_hbm, nkv_hbm, pre_hbm, dec_hbm, plen, dlen, wo_hbm, barrier):
    r, c, n, dec, span = d["rows"], d["chips"], 2 * d["chips"], d["dec"], d["rows"] - d["dec"]
    hq, per_kv, hd_dev, ctx, pre_dev = d["heads_q"], d["per_kv"], d["heads_dev"], d["ctx"], d["pre_dev"]
    jw, half = hd_dev * HD, d["model"] // 2
    t = 2 * y + k
    other = 1 - k
    scale = HD ** -0.5
    l_sem = S["l_sem"]

    def local(src, dst, i):
        copy = pltpu.make_async_copy(src, dst, l_sem.at[i])
        copy.start()
        return copy

    kv_cols = cols(y * HD, HD)
    l_n = local(nkv_hbm, S["nkv_v"], 0)
    l_p = local(pre_hbm.at[:, 0], S["pre_v"], 1)
    l_q = local(q_hbm, S["q_v"], 2)
    l_own = [
        local(nkv_hbm.at[:, :, kv_cols], S["kvn"].at[k, y], 3),
        local(pre_hbm.at[:, 0, :, kv_cols], S["kvp"].at[k, y], 4),
        local(q_hbm.at[:, cols(t * jw, jw)], S["qb"].at[t], 5),
    ]
    l_d = local(dec_hbm, S["dec_v"], 6)
    l_w = local(wo_hbm.at[:, cols(k * half, half)], S["wo"].at[k], 7)

    barrier()

    def kn_copy(src_y, to):
        return remote(
            S["nkv_v"].at[:, :, cols(to * HD, HD)], S["kvn"].at[k, src_y],
            S["kns_sem"].at[to], S["knr_sem"].at[src_y], **{CHIP: to},
        )

    def kp_copy(src_y, to):
        return remote(
            S["pre_v"].at[:, :, cols(to * HD, HD)], S["kvp"].at[k, src_y],
            S["kps_sem"].at[to], S["kpr_sem"].at[src_y], **{CHIP: to},
        )

    def q_copy(src_t, to_t):
        return remote(
            S["q_v"].at[:, cols(to_t * jw, jw)], S["qb"].at[src_t],
            S["qs_sem"].at[to_t], S["qr_sem"].at[src_t], **{CHIP: to_t // 2, CORE: to_t % 2},
        )

    l_n.wait()
    l_p.wait()
    for o in range(1, c):
        to = lax.rem(y + ((o + 1) // 2 if o % 2 else c - o // 2), c)
        copies.start(kn_copy(y, to))
        copies.start(kp_copy(y, to))
    l_q.wait()
    for o in range(c):
        to = y if o == 0 else lax.rem(y + ((o + 1) // 2 if o % 2 else c - o // 2), c)
        for kk in ([1] if o == 0 else [0, 1]):
            to_k = lax.rem(k + kk, 2)
            copies.start(q_copy(t, 2 * to + to_k))
    wo_copy = copies.start(remote(
        wo_hbm.at[:, cols(other * half, half)], S["wo"].at[k], S["x_s"].at[0], S["x_r"].at[0],
        **{CORE: other},
    ))

    l_d.wait()
    q8 = S["q_v"][16:24, :].astype(F32)
    n8 = [S["nkv_v"][i, 16:24, :].astype(F32) for i in range(2)]
    m = per_kv * 8
    keys = dec * ctx
    lane = iota((m, keys), 1)
    row8 = iota((m, keys), 0) & 7
    req = sum((lane >= ctx * i).astype(jnp.int32) for i in range(1, dec))
    pos = lane - ctx * req
    length = dlen[0]
    for i in range(1, dec):
        length = jnp.where(req == i, dlen[i], length)
    seen = (row8 - (8 - dec) == req) & (pos < length)
    for g in range(hq // per_kv):
        qg = jnp.concatenate(
            [q8[:, (g * per_kv + h) * HD : (g * per_kv + h + 1) * HD] for h in range(per_kv)], axis=0
        )
        kg = S["dec_v"][0, :, :, g * HD : (g + 1) * HD].reshape(keys, HD)
        vg = S["dec_v"][1, :, :, g * HD : (g + 1) * HD].reshape(keys, HD)
        own_k = jnp.concatenate([n8[0][:, g * HD : (g + 1) * HD]] * per_kv, axis=0)
        own_v = jnp.concatenate([n8[1][:, g * HD : (g + 1) * HD]] * per_kv, axis=0)
        s = jnp.where(seen, dot_t(qg.astype(BF16), kg) * scale, NEG)
        s_own = jnp.sum(qg * own_k, axis=1, keepdims=True) * scale
        top = jnp.maximum(jnp.max(s, axis=1, keepdims=True), s_own)
        p = jnp.where(seen, jnp.exp(s - top), 0.0)
        p_own = jnp.exp(s_own - top)
        den = jnp.sum(p, axis=1, keepdims=True) + p_own
        o = dot(p.astype(BF16), vg) + p_own.astype(BF16).astype(F32) * own_v
        S["dec_o"][g * m : (g + 1) * m, :] = (o / den).astype(BF16)
    to_row = iota((n * 16, hq * 8), 0)
    from_row = iota((n * 16, hq * 8), 1)
    slot = to_row & 15
    wanted = (to_row >> 4) * (8 * hd_dev) + (slot >> 2) * 8 + (8 - dec) + (slot & 3)
    pick = ((from_row == wanted) & (slot < hd_dev * dec)).astype(BF16)
    S["decs"][...] = dot(pick, S["dec_o"][...]).astype(BF16).reshape(n, 16, HD)

    def d_copy(src_t, to_t):
        return remote(
            S["decs"].at[to_t], S["decr"].at[src_t],
            S["ds_sem"].at[to_t], S["dr_sem"].at[src_t], **{CHIP: to_t // 2, CORE: to_t % 2},
        )

    for o in range(1, n):
        copies.start(d_copy(t, lax.rem(t + o, n)))
    S["decr"][t] = S["decs"][t]

    for copy in l_own:
        copy.wait()
    for o in range(1, c):
        src = lax.rem(y + o, c)
        kn_copy(src, y).wait_recv()
        kp_copy(src, y).wait_recv()
    relay = [
        copies.start(remote(S[b].at[k], S[b].at[k], S["x_s"].at[i], S["x_r"].at[i], **{CORE: other}))
        for i, b in ((1, "kvn"), (2, "kvp"))
    ]
    for o in range(1, n):
        q_copy(lax.rem(t + o, n), t).wait_recv()
    for cc in range(c):
        pair = [S["qb"][2 * cc + i].astype(F32) for i in range(2)]
        for j in range(hd_dev):
            S["qh"][j * n * r + cc * 2 * r : j * n * r + (cc + 1) * 2 * r, :] = jnp.concatenate(
                [q[:, j * HD : (j + 1) * HD] for q in pair], axis=0
            ).astype(BF16)
    for copy in relay:
        copy.wait_recv()
    prefix = n * pre_dev
    for i, b in ((0, "kall"), (1, "vall")):
        for cc in range(c):
            for kk in range(2):
                at = (2 * cc + kk) * pre_dev
                S[b][at : at + pre_dev, :] = S["kvp"][kk, cc, i]
            S[b][prefix + cc * 2 * r : prefix + (cc + 1) * 2 * r, :] = jnp.concatenate(
                [S["kvn"][kk, cc, i].astype(F32) for kk in range(2)], axis=0
            ).astype(BF16)
    for o in range(1, n):
        d_copy(lax.rem(t + o, n), t).wait_recv()

    block_devs = 4
    block = block_devs * r
    col = iota((1, n * r), 1)
    col_dev = sum((col >= r * i).astype(jnp.int32) for i in range(1, n))
    col_in = col - r * col_dev
    key_place = jnp.where(col_in < span, col_dev * span + col_in, 1 << 20)
    pre_seen = iota((1, prefix), 1) < plen[0]
    row = iota((block, 1), 0)
    row_dev = sum((row >= r * i).astype(jnp.int32) for i in range(1, block_devs))
    row_in = row - r * row_dev
    from_col = iota((block, n * 16), 1)

    def attend(b, carry):
        device = b * block_devs + row_dev
        place = device * span + row_in
        new_seen = key_place <= place
        first = b * block
        for j in range(hd_dev):
            q = S["qh"][rows(j * n * r + first, block, 16), :]
            s1 = jnp.where(pre_seen, dot_t(q, S["kall"][:prefix, :]) * scale, NEG)
            s2 = jnp.where(new_seen, dot_t(q, S["kall"][prefix:, :]) * scale, NEG)
            top = jnp.maximum(jnp.max(s1, axis=1, keepdims=True), jnp.max(s2, axis=1, keepdims=True))
            p1 = jnp.exp(s1 - top)
            p2 = jnp.exp(s2 - top)
            den = jnp.sum(p1, axis=1, keepdims=True) + jnp.sum(p2, axis=1, keepdims=True)
            o = (dot(p1.astype(BF16), S["vall"][:prefix, :]) + dot(p2.astype(BF16), S["vall"][prefix:, :])) / den
            wanted = jnp.where(row_in >= span, device * 16 + j * dec + row_in - span, -1)
            own = dot((from_col == wanted).astype(BF16), S["decr"][...].reshape(n * 16, HD))
            S["att"][k, rows(first, block, 16), j * HD : (j + 1) * HD] = jnp.where(
                row_in < span, o, own
            ).astype(BF16)
        return carry

    lax.fori_loop(0, n // block_devs, attend, 0)
    att_copy = copies.start(remote(
        S["att"].at[k], S["att"].at[k], S["x_s"].at[3], S["x_r"].at[3], **{CORE: other},
    ))
    l_w.wait()
    wo_copy.wait_recv()
    att_copy.wait_recv()

    width = 256

    def project(i, carry):
        at = cols(i * width, width)
        S["part"][:, at] = dot(S["att"][0], S["wo"][0, :, at]) + dot(S["att"][1], S["wo"][1, :, at])
        return carry

    lax.fori_loop(0, half // width, project, 0)
    quarter = half // 2

    def share(dest, h, sub):
        return S["part"][rows(dest * 2 * r, 2 * r, 16), h * quarter : (h + 1) * quarter]

    total = ring_reduce(y, c, copies, share, S["rs_out"], S["rs_in"], S["rs_s"], S["rs_r"], 1)
    return [total(h, 0) for h in range(2)]


def entry_barrier(y, k, chips, x=None, groups=0):
    def greet():
        barrier = pltpu.get_barrier_semaphore()
        for o in range(chips):
            for kk in ([1] if o == 0 else [0, 1]):
                pl.semaphore_signal(
                    barrier, inc=1,
                    device_id={CHIP: lax.rem(y + o, chips), CORE: lax.rem(k + kk, 2)},
                    device_id_type=MESH,
                )
        for o in range(1, groups):
            pl.semaphore_signal(
                barrier, inc=1, device_id={EXP: lax.rem(x + o, groups)}, device_id_type=MESH
            )
        pl.semaphore_wait(barrier, 2 * chips - 1 + max(groups - 1, 0))

    return greet


def k1_only(d, names, *refs):
    q, nkv, pre, dec, plen, dlen, wo, out, *rest = refs
    S = dict(zip(names, rest))
    y, k = lax.axis_index(CHIP), lax.axis_index(CORE)
    copies = Copies()
    got = attend_and_project(d, S, y, k, copies, q, nkv, pre, dec, plen, dlen, wo, entry_barrier(y, k, d["chips"]))
    r = d["rows"]
    mine = jnp.concatenate(got, axis=1)
    S["fin"][k] = mine
    copy = copies.start(remote(S["fin"].at[k], S["fin"].at[k], S["x_s"].at[4], S["x_r"].at[4], **{CORE: 1 - k}))
    copy.wait_recv()
    half = d["model"] // 2
    out[:, :half] = S["fin"][0, rows(k * r, r, 8), :]
    out[:, half:] = S["fin"][1, rows(k * r, r, 8), :]
    copies.drain()


def dims(hidden_in, queries, new_kv, prefix_kv, decode_kv, decode_len):
    kvw = new_kv.shape[2]
    chips = lax.axis_size(CHIP)
    hq = queries.shape[1] // HD
    return dict(
        rows=hidden_in.shape[0], model=hidden_in.shape[1], kvw=kvw, chips=chips, heads_q=hq,
        per_kv=hq // (kvw // HD), heads_dev=hq // (2 * chips), pre_dev=prefix_kv.shape[2],
        dec=decode_len.shape[0], ctx=decode_kv.shape[2],
    )


def run_k1(d, queries, new_kv, prefix_kv, decode_kv, prefix_len, decode_len, out_proj):
    scratch = k1_scratch(d)
    scratch["fin"] = pltpu.VMEM((2, 2 * d["rows"], d["model"] // 2), F32)
    names = list(scratch)
    anys = pl.BlockSpec(memory_space=pl.ANY)
    smem = pl.BlockSpec(memory_space=pltpu.SMEM)

    def kernel(*refs):
        k1_only(d, names, *refs)

    return pl.pallas_call(
        kernel,
        out_shape=jax.ShapeDtypeStruct((d["rows"], d["model"]), F32),
        in_specs=[anys] * 4 + [smem] * 2 + [anys],
        out_specs=pl.BlockSpec(memory_space=pltpu.VMEM),
        scratch_shapes=list(scratch.values()),
        compiler_params=pltpu.CompilerParams(collective_id=0, has_side_effects=True),
        name="attend",
    )(queries, new_kv, prefix_kv, decode_kv, prefix_len, decode_len, out_proj)


def on_device(
    hidden_in,
    queries,
    new_kv,
    prefix_kv,
    decode_kv,
    prefix_len,
    decode_len,
    out_proj,
    norm_gain,
    router_w,
    expert_ids,
    w_gate,
    w_up,
    w_down,
):
    groups = lax.axis_size("exp")
    rows_dev, model_width = hidden_in.shape
    d = dims(hidden_in, queries, new_kv, prefix_kv, decode_kv, decode_len)
    projected = run_k1(d, queries, new_kv, prefix_kv, decode_kv, prefix_len, decode_len, out_proj)
    residual = hidden_in.astype(jnp.float32) + projected
    mean_square = jnp.mean(residual * residual, axis=1, keepdims=True)
    normed = (residual * lax.rsqrt(mean_square + 1e-05) * norm_gain).astype(jnp.bfloat16)
    logits = jnp.dot(normed, router_w, preferred_element_type=jnp.float32)
    experts = router_w.shape[1]
    chosen_hot = (expert_ids[:, :, None] == jnp.arange(experts, dtype=jnp.int32)).astype(jnp.int32)
    chosen_logits = jnp.sum(jnp.where(chosen_hot == 1, logits[:, None, :], 0.0), axis=2)
    route_weights = jax.nn.softmax(chosen_logits, axis=1)
    flat_hot = chosen_hot.reshape(rows_dev * 2, experts)
    slot_rank = jnp.sum((jnp.cumsum(flat_hot, axis=0) - flat_hot) * flat_hot, axis=1).reshape(
        rows_dev, 2
    )
    capacity = CAP
    slot_index = jnp.arange(capacity, dtype=jnp.int32)
    assignment = chosen_hot[:, :, :, None] * (slot_rank[:, :, None, None] == slot_index).astype(
        jnp.int32
    )
    placement = jnp.sum(assignment, axis=1)
    local_experts = experts // groups
    placement_split = placement.reshape(rows_dev, groups, local_experts, capacity).astype(
        jnp.bfloat16
    )
    outgoing = jnp.einsum(
        "rnlc,rd->lncd", placement_split, normed, preferred_element_type=jnp.float32
    ).astype(jnp.bfloat16)
    arrived = lax.all_to_all(outgoing, "exp", split_axis=1, concat_axis=1, tiled=True)
    shard_rows = lax.all_gather(arrived, TEN, axis=1, tiled=True)
    gate_act = jnp.einsum("lscd,ldf->lscf", shard_rows, w_gate, preferred_element_type=jnp.float32)
    up_act = jnp.einsum("lscd,ldf->lscf", shard_rows, w_up, preferred_element_type=jnp.float32)
    hidden = (jax.nn.silu(gate_act) * up_act).astype(jnp.bfloat16)
    row_block = hidden
    summed = lax.psum_scatter(
        jnp.einsum("lscf,lfd->slcd", row_block, w_down, preferred_element_type=jnp.float32).astype(
            jnp.bfloat16
        ),
        TEN,
        scatter_dimension=0,
        tiled=True,
    )
    returned = lax.all_to_all(summed, "exp", split_axis=0, concat_axis=0, tiled=True)
    outputs = returned.reshape(experts * capacity, model_width).astype(jnp.float32)
    weight_map = jnp.sum(
        assignment.astype(jnp.float32) * route_weights[:, :, None, None], axis=1
    ).reshape(rows_dev, experts * capacity)
    expert_mix = jnp.dot(weight_map, outputs, preferred_element_type=jnp.float32)
    return (residual + expert_mix).astype(jnp.bfloat16)


def solution(mesh):
    split = Mesh(
        mesh.devices.reshape(mesh.shape["rep"], mesh.shape["exp"], mesh.shape["ten"] // 2, 2),
        ("rep", "exp", "ten_0", "ten_1"),
    )
    return jax.shard_map(
        on_device,
        mesh=split,
        in_specs=(
            P(REP_EXP_TEN, None),
            P(REP_EXP_TEN, None),
            P(None, REP_EXP_TEN, None),
            P(None, ("rep", "exp"), TEN, None),
            P(None, REP_EXP_TEN, None, None),
            P(("rep", "exp")),
            P(REP_EXP_TEN),
            P(TEN, None),
            P(),
            P(),
            P(REP_EXP_TEN, None),
            P("exp", None, TEN),
            P("exp", None, TEN),
            P("exp", TEN, None),
        ),
        out_specs=P(REP_EXP_TEN, None),
        check_vma=False,
    )
```

time: 363 us -> 264 us (0.73)
  waiting for transfers between devices: 214 us -> 118 us
  Pallas kernels: 0 us -> 68.4 us
  local copies, waits for them, and re-layouts: 48.2 us -> 12.2 us
  blocking collectives: 33.9 us -> 17.6 us
  matrix products: 32.7 us -> 21.8 us
  other arithmetic: 11.4 us -> 3.47 us
    pallas_call x0 -> x1, Pallas kernels: none -> 68.4 us  [run_k1(): pl.pallas_call(kernel, out_shape=jax.ShapeDtypeStruct((d['rows'], d['mode...]
    reduce_scatter x2 -> x0, waiting for transfers between devices: 53.1 us -> none  [the longest x1 38.8 us: sum_by_chip(): return lax.psum_scatter(parts, chips, scatter_dimension=0, tiled=True)[0]]
    all_gather x1 -> x0, waiting for transfers between devices: 46.6 us -> none  [one_gather(): lines, at, done = (lax.all_gather(line, axis), 0, [])]
    all_to_all x1 -> x0, blocking collectives: 16.7 us -> none  [on_device(): lax.all_to_all(attended_rows, TEN, split_axis=1, concat_axis=0, tiled=True)]
    concatenate x11 -> x0, local copies, waits for them, and re-layouts: 12.3 us -> none  [the longest x3 5.37 us: on_device(): jnp.concatenate([full_prefix[1], full_fresh[1]], axis=0)]
    slice x10 -> x0, local copies, waits for them, and re-layouts: 9.71 us -> none  [the longest x1 2.65 us: on_device(): full_fresh[1]]
    dot_general x4 -> x0, matrix products: 8.66 us -> none  [the longest x1 3.07 us: on_device(): jnp.dot(row_block, out_proj, preferred_element_type=jnp.float32)]
    all_to_all x1, waiting for transfers between devices: 5.13 us -> 9.67 us  [on_device(): lax.all_to_all(summed, 'exp', split_axis=0, concat_axis=0, tiled=True)]
  transfers between devices with their start and end apart: 6 -> 3, of which waited for: 6 -> 3; matrix products, arithmetic and copies ran while one was open for 6% -> 0% of each run, Pallas kernels for 0% -> 0%
where the time goes in v1:
time: 264 us; the launch traced here: 261 us
  waiting for transfers between devices  118 us (45%)
  Pallas kernels  68.4 us (26%)
  matrix products  21.8 us (8%)
  blocking collectives  17.6 us (7%)
  between operations  14.2 us (5%)
  local copies, waits for them, and re-layouts  12.2 us (5%)
  starting transfers between devices  5.71 us (2%)
  other arithmetic  3.47 us (1%)
    pallas_call x1, Pallas kernels, run_k1(): pl.pallas_call(kernel, out_shape=jax.ShapeDtypeStruct((d['rows'], d['mode...  68.4 us
    unnamed x3, waiting for transfers between devices  63.2 us
    all_gather x1, waiting for transfers between devices, on_device(): shard_rows = lax.all_gather(arrived, TEN, axis=1, tiled=True)  45 us
    all_to_all x1, blocking collectives, on_device(): lax.all_to_all(outgoing, 'exp', split_axis=1, concat_axis=1, tiled=True)  17.6 us
    dot_general x1, matrix products, on_device(): jnp.einsum('lscf,lfd->slcd', row_block, w_down, preferred_element_type=jn...  10.9 us
    all_to_all x1, waiting for transfers between devices, on_device(): lax.all_to_all(summed, 'exp', split_axis=0, concat_axis=0, tiled=True)  9.67 us
    dot_general x1, matrix products, on_device(): jnp.einsum('lscd,ldf->lscf', shard_rows, w_gate, preferred_element_type=j...  7.77 us
    unnamed x16, local copies, waits for them, and re-layouts  6.93 us
  transfers between devices with their start and end apart: 3, of which 3 were waited for; matrix products, arithmetic and copies ran while one was open for 0% of the time, Pallas kernels for 0%

profile of v1, /device:TPU:513, one launch (start us, length us, event | category | flops | bytes accessed | tf_op | source)
XLA Modules:
  0.0 261.2 jit_solution(11271996918533632089)
XLA Ops:
  6.5 0.0 copy-start
  6.6 0.0 copy-start.3
  6.6 0.0 copy-start.5
  6.6 0.0 all-gather.2.cloned.1.call-start
  6.6 0.8 fusion.22
  7.4 0.9 copy.28
  9.0 0.1 eq.55
  9.0 0.1 fusion.20
  9.1 0.1 reduce_window_sum.11
  9.2 0.2 select_reduce_fusion
  9.4 0.1 eq.59
  9.5 0.1 copy.29
  9.6 68.4 %attend.1 = f32[24,3072]{1,0:T(8,128)} custom-call(bf16[24,6144]{1,0:T(8,128)(2,1)} %refs_0_.1, bf16[2,24,1024]{2,1,0:T(8,128)(2,1)} %refs_1_.1, bf16[2,1,32,1024]{3,2,1,0:T(8,128)(2,1)} %refs_2_.1, bf16[2,4,48,1024]{3,2,1,0:T(8,128)(2,1)} %refs_3_.1, s32[1]{0:T(128)S(6)} %copy.38.refs_4_, s32[4]{0:T(128)} %refs_5_.1, bf16[384,3072]{1,0:T(8,128)(2,1)} %refs_6_.1), custom_call_target="tpu_custom_call" | custom-call | tf_op jit(solution)/shard_map/attend/pallas_call | solution.py:402
  78.0 0.0 copy-done.3
  78.0 1.1 multiply_reduce_fusion
  79.2 0.0 copy-done.5
  79.2 1.1 multiply_convert_fusion.1
  80.2 0.0 copy-start.2
  80.3 0.7 copy-done.2
  80.9 0.2 fusion.4
  81.1 0.2 copy.31
  81.4 17.6 %all_to_all.10 = bf16[1,8,7,3072]{3,2,0,1:T(8,128)(2,1)S(1)} all-to-all(bf16[1,8,7,3072]{3,2,0,1:T(8,128)(2,1)S(1)} %copy.31), channel_id=1, replica_groups=mesh['rep'=2,'exp'=8,'ten_0'=8,'ten_1'=2] {'exp'}, dimensions={1} | all-to-all | bytes 688128 | tf_op jit(solution)/shard_map/all_to_all | solution.py:458
  98.9 1.0 copy.32
  99.9 0.1 all-gather.2.cloned.1.call-update
  100.0 0.1 reduce-scatter.4.cloned.1.call-start
  100.0 45.0 %all-gather.2.cloned.1.call-done = bf16[1,128,7,3072]{3,1,2,0:T(8,128)(2,1)} async-done(((bf16[1,8,7,3072]{3,1,2,0:T(8,128)(2,1)}), bf16[1,128,7,3072]{3,1,2,0:T(8,128)(2,1)}) %all-gather.2.cloned.1.call-update) | async-done | bytes 5505040 | tf_op jit(solution)/shard_map/all_gather | solution.py:459
  145.0 7.8 %fusion.2 = f32[128,7,512]{2,0,1:T(8,128)} fusion(bf16[1,128,7,3072]{3,1,2,0:T(8,128)(2,1)} %all-gather.2.cloned.1.call-done, bf16[1,3072,512]{2,1,0:T(8,128)(2,1)} %param.25), kind=kOutput, calls=%fused_computation.2 | convolution fusion | flops 2818572288 | bytes 10485760 | tf_op jit(solution)/shard_map/lscd,ldf->lscf/dot_general | solution.py:460
  152.8 0.0 copy-done
  152.8 10.9 %fusion.27 = bf16[16,8,7,3072]{3,1,0,2:T(8,128)(2,1)} fusion(bf16[1,512,3072]{2,1,0:T(8,128)(2,1)S(1)} %copy-done, f32[128,7,512]{2,0,1:T(8,128)} %fusion.2, bf16[1,3072,512]{2,1,0:T(8,128)(2,1)} %param.26, bf16[1,128,7,3072]{3,1,2,0:T(8,128)(2,1)} %all-gather.2.cloned.1.call-done), kind=kOutput, calls=%fused_computation.35 | convolution fusion | flops 5642649600 | bytes 19136512 | tf_op jit(solution)/shard_map/lscf,lfd->slcd/dot_general | solution.py:465
  163.6 5.3 %copy.36 = bf16[16,8,7,3072]{3,1,2,0:T(8,128)(2,1)} copy(bf16[16,8,7,3072]{3,1,0,2:T(8,128)(2,1)} %fusion.27) | data formatting | bytes 11010048
  169.0 0.0 copy-start.4
  169.0 0.0 copy-start.6
  169.0 0.0 copy-start.1
  169.0 0.1 reduce-scatter.4.cloned.1.call-update
  169.0 63.1 %reduce-scatter.4.cloned.1.call-done = bf16[8,21504]{1,0:T(8,128)(2,1)} async-done(((bf16[128,21504]{1,0:T(8,128)(2,1)}), bf16[8,21504]{1,0:T(8,128)(2,1)}) %reduce-scatter.4.cloned.1.call-update) | async-done | bytes 344080
  232.2 1.9 copy.33
  234.1 5.6 %all-to-all-start.1 = ((bf16[8,1,7,3072]{3,2,1,0:T(8,128)(2,1)}), bf16[8,1,7,3072]{3,2,1,0:T(8,128)(2,1)}, u32[]{:S(2)}, u32[]{:S(2)}) async-start(bf16[8,1,7,3072]{3,2,1,0:T(8,128)(2,1)} %copy.33), calls=%async_computation.1 | async-start | bytes 786432 | tf_op jit(solution)/shard_map/all_to_all | solution.py:472
  239.7 0.0 copy-done.4
  239.7 1.1 fusion.34
  240.8 0.0 copy-done.6
  240.9 9.7 %all-to-all-done.1 = bf16[8,1,7,3072]{3,2,1,0:T(8,128)(2,1)} async-done(((bf16[8,1,7,3072]{3,2,1,0:T(8,128)(2,1)}), bf16[8,1,7,3072]{3,2,1,0:T(8,128)(2,1)}, u32[]{:S(2)}, u32[]{:S(2)}) %all-to-all-start.1) | async-done | bytes 344096 | tf_op jit(solution)/shard_map/all_to_all | solution.py:472
  250.6 1.9 reshape.105
  252.5 0.0 copy-done.1
  252.5 1.9 fusion.5
  (10 shorter events, 0.2 us)
Async XLA Ops:
  6.5 146.2 %copy-start = (bf16[1,512,3072]{2,1,0:T(8,128)(2,1)S(1)}, bf16[1,512,3072]{2,1,0:T(8,128)(2,1)}, u32[]{:S(2)}) copy-start(bf16[1,512,3072]{2,1,0:T(8,128)(2,1)} %param.27) | copy-start | bytes 9437188
  6.6 71.5 %copy-start.3 = (bf16[24,3072]{1,0:T(8,128)(2,1)S(1)}, bf16[24,3072]{1,0:T(8,128)(2,1)}, u32[]{:S(2)}) copy-start(bf16[24,3072]{1,0:T(8,128)(2,1)} %param.14) | copy-start | bytes 442372
  6.6 72.6 %copy-start.5 = (f32[3072]{0:T(1024)S(1)}, f32[3072]{0:T(1024)}, u32[]{:S(2)}) copy-start(f32[3072]{0:T(1024)} %param.22) | copy-start | bytes 36868
  6.6 138.4 %all-gather.2.cloned.1.call-start = ((), (), s32[]{:S(2)}) async-start(), calls=%async_computation.3 | async-start | bytes 5849088 | tf_op jit(solution)/shard_map/all_gather | solution.py:459
  80.2 0.7 copy-start.2
  100.0 132.2 %reduce-scatter.4.cloned.1.call-start = ((), (), s32[]{:S(2)}) async-start(), calls=%async_computation.4 | async-start | bytes 5849088
  169.0 70.8 %copy-start.4 = (bf16[3072,8]{0,1:T(8,128)(2,1)S(1)}, bf16[3072,8]{0,1:T(8,128)(2,1)}, u32[]{:S(2)}) copy-start(bf16[3072,8]{0,1:T(8,128)(2,1)} %param.23) | copy-start | bytes 147460
  169.0 71.8 %copy-start.6 = (s32[24,2]{0,1:T(2,128)S(1)}, s32[24,2]{0,1:T(2,128)}, u32[]{:S(2)}) copy-start(s32[24,2]{0,1:T(2,128)} %param.24) | copy-start | bytes 580
  169.0 83.5 %copy-start.1 = (f32[24,3072]{1,0:T(8,128)S(1)}, f32[24,3072]{1,0:T(8,128)}, u32[]{:S(2)}) copy-start(f32[24,3072]{1,0:T(8,128)} %attend.1) | copy-start | bytes 884740
  234.1 16.5 %all-to-all-start.1 = ((bf16[8,1,7,3072]{3,2,1,0:T(8,128)(2,1)}), bf16[8,1,7,3072]{3,2,1,0:T(8,128)(2,1)}, u32[]{:S(2)}, u32[]{:S(2)}) async-start(bf16[8,1,7,3072]{3,2,1,0:T(8,128)(2,1)} %copy.33), calls=%async_computation.1 | async-start | bytes 786432 | tf_op jit(solution)/shard_map/all_to_all | solution.py:472
Sparse Core Ops, SparseCore 0:
  100.1 44.8 all-gather.1
  169.2 62.9 reduce-scatter.3
